TPU v7x, 32 devices: a whole 2x2x4 slice. The times are simulated.
32 devices in a mesh: dom: 16 (over z, y, x), feat: 2 (over core).
Axes of the slice: x: 2, y: 2, z: 4, core: 2. Of those that a mesh axis runs over, the one named last changes fastest.
Arguments:
- features: bfloat16 [32768, 608], P('dom', 'feat'), may hold values from -6 to 6
- weight: bfloat16 [608, 256], replicated, may hold values from -0.25 to 0.25
- out_bias: float32 [256], P('feat'), may hold values from -3 to 3
- tile_values: bfloat16 [1728, 128, 128], P('dom'), may hold values from -0.25 to 0.25
- tile_rows: int32 [1728], P('dom'), may hold values from 0 to 15
- tile_cols: int32 [1728], P('dom'), may hold values from 0 to 81, as said below
- tile_count: int32 [16], P('dom'), may hold values from 10 to 108, as said below
- send_rows: int32 [16, 8, 1024], P('dom'), may hold values from 0 to 2047
- hub_ids: int32 [256], replicated, may hold values from 0 to 32767, as said below
Outputs:
- activations: bfloat16 [32768, 256], P('dom', 'feat')
Inputs may be any that keep to these rules, and one draw needn't show every extreme that they name: `tile_count`: slots at or past a partition's count are not part of the graph; some partition uses all 108 slots. `tile_cols`: column blocks index the extended row space of the slot's partition. `hub_ids`: distinct vertex ids; vertex v belongs to partition v // 2048; no partition owns more than 48 hubs, and some partition owns exactly 48.
All inputs are finite; a program needn't handle non-finite values.
Results may differ from a plain program's by a relative error of at most 0.0044.
Values may be sent and summed in bfloat16 or wider, within the bound.
A program may use at most 64 MiB of HBM per device.

v0:
```python
import functools
import math

import jax
import jax.numpy as jnp
from jax import lax
from jax.experimental import pallas as pl
from jax.experimental.pallas import tpu as pltpu
from jax.sharding import PartitionSpec as P

REACH = 4
HUB_MOST = 48


def passed_along(value, axis, steps):
    count = lax.axis_size(axis)
    initial, last = (max(0, -steps), min(count, count - steps))
    return lax.ppermute(value, axis, [(source, source + steps) for source in range(initial, last)])


def local_any(
    features, weight, out_bias, tile_values, tile_rows, tile_cols, tile_count, send_rows, hub_ids
):
    column_count = out_bias.shape[0]
    vertex_rows = features.shape[0]
    part_index = lax.axis_index("dom")
    feat_index = lax.axis_index("feat")
    weight_cols = lax.dynamic_slice_in_dim(weight, feat_index * column_count, column_count, 1)
    summed = jnp.dot(
        lax.all_gather(features, "feat", axis=1, tiled=True),
        weight_cols,
        preferred_element_type=jnp.float32,
    )
    projected = summed.astype(jnp.bfloat16)
    half_rows = send_rows.shape[2]
    slot_total = send_rows.shape[1]
    offsets = list(range(-REACH, 0)) + list(range(1, REACH + 1))
    packed_all = projected[send_rows[0].reshape(slot_total * half_rows)].reshape(
        slot_total, half_rows, column_count
    )
    received = []
    for slot_index, offset_value in enumerate(offsets):
        received.append(passed_along(packed_all[slot_index], "dom", offset_value))
    halo_block = jnp.concatenate(received, 0)
    owners = hub_ids // vertex_rows
    mine = owners == part_index
    local_index = jnp.clip(hub_ids - part_index * vertex_rows, 0, vertex_rows - 1)
    candidates = projected[local_index]
    hub_total = hub_ids.shape[0]
    positions = jnp.arange(hub_total, dtype=jnp.int32)
    earlier = (owners[:, None] == owners[None, :]) & (positions[:, None] > positions[None, :])
    ranks = jnp.sum(earlier.astype(jnp.int32), 1)
    selector = (
        mine[:, None] & (ranks[:, None] == jnp.arange(HUB_MOST, dtype=jnp.int32)[None, :])
    ).astype(jnp.bfloat16)
    slot_rows = lax.dot_general(
        selector, candidates, (((0,), (0,)), ((), ())), preferred_element_type=jnp.float32
    ).astype(jnp.bfloat16)
    gathered = lax.all_gather(slot_rows, "dom", axis=0, tiled=True)
    hub_block = gathered[owners * HUB_MOST + ranks]
    extended = jnp.concatenate([projected, halo_block, hub_block], 0)
    block_edge = tile_values.shape[1]
    blocks = extended.reshape(extended.shape[0] // block_edge, block_edge, column_count)
    products = jnp.einsum(
        "tij,tjc->tic", tile_values, blocks[tile_cols], preferred_element_type=jnp.float32
    )
    live_mask = jnp.arange(tile_values.shape[0], dtype=jnp.int32) < tile_count[0]
    block_count = vertex_rows // block_edge
    assignment = (
        (tile_rows[None, :] == jnp.arange(block_count, dtype=jnp.int32)[:, None])
        & live_mask[None, :]
    ).astype(jnp.float32)
    aggregate = jnp.einsum("rt,tic->ric", assignment, products, precision=lax.Precision.HIGHEST)
    activated = jnp.maximum(aggregate + out_bias[None, None, :], 0.0).astype(jnp.bfloat16)
    return activated.reshape(vertex_rows, column_count)

LANES = 128
GROUPS = 4
PLANE = 4
MESH = pl.DeviceIdType.MESH


def picked_rows(index, table_ref, groups):
    depth = table_ref.shape[0]
    group = index // depth
    within = index - group * depth
    positions = lax.broadcasted_iota(jnp.int32, (index.shape[0], depth), 1)
    chosen = (positions == within).astype(jnp.float32).astype(jnp.bfloat16)
    every = jnp.dot(chosen, table_ref[...], preferred_element_type=jnp.float32)
    width = table_ref.shape[1] // groups
    result = every[:, :width]
    for number in range(1, groups):
        part = every[:, number * width : (number + 1) * width]
        result = jnp.where(group == number, part, result)
    return result.astype(jnp.bfloat16)


def over_rows(left, right):
    dims = (((0,), (0,)), ((), ()))
    return lax.dot_general(left, right, dims, preferred_element_type=jnp.float32)


def exchange_kernel(
    count, features_ref, weight_ref, send_ref, hub_ref, extended_ref,
    other_ref, total_ref, table_ref, index_ref, packed_ref, own_hubs_ref, hubs_ref,
    feature_sems, send_sems, receive_sems, hub_send_sems, hub_receive_sems,
):
    part = lax.axis_index("dom")
    feat = lax.axis_index("feat")
    depth, vertex_rows = features_ref.shape
    width = extended_ref.shape[1]
    lines = count // PLANE
    line = part // PLANE
    group_rows = vertex_rows // GROUPS
    slots, half_rows = send_ref.shape
    offsets = list(range(-REACH, 0)) + list(range(1, REACH + 1))
    hub_total = hub_ref.shape[1]
    halo_end = vertex_rows + slots * half_rows

    barrier = pltpu.get_barrier_semaphore()
    pl.semaphore_signal(barrier, inc=1, device_id=(part, 1 - feat), device_id_type=MESH)

    def greet(step, carry):
        peer = lax.rem(part + step * PLANE, count)
        pl.semaphore_signal(barrier, inc=1, device_id=(peer, feat), device_id_type=MESH)
        return carry

    lax.fori_loop(1, lines, greet, 0)
    greeted = lines
    for offset in offsets:
        if abs(offset) % PLANE != 0:
            target = part + offset
            inside = (target >= 0) & (target < count)
            greeted = greeted + inside.astype(jnp.int32)

            @pl.when(inside)
            def _():
                pl.semaphore_signal(
                    barrier, inc=1, device_id=(target, feat), device_id_type=MESH
                )

    columns = pl.ds(pl.multiple_of(feat * width, width), width)
    own_weight = weight_ref[pl.ds(pl.multiple_of(feat * depth, 16), depth), columns]
    other_weight = weight_ref[pl.ds(pl.multiple_of((1 - feat) * depth, 16), depth), columns]
    total_ref[...] = over_rows(own_weight, features_ref[...])
    index_ref[...] = jnp.transpose(send_ref[...])

    hub_row = hub_ref[...]
    hub_col = jnp.transpose(jnp.broadcast_to(hub_row, (8, hub_total)))[:, :1]
    owner_row = hub_row // vertex_rows
    owner_col = hub_col // vertex_rows
    same = owner_row == owner_col
    first = lax.broadcasted_iota(jnp.int32, (hub_total, hub_total), 0)
    second = lax.broadcasted_iota(jnp.int32, (hub_total, hub_total), 1)
    rank_row = jnp.sum(jnp.where(same & (first < second), 1.0, 0.0), 0, keepdims=True)
    rank_col = jnp.sum(jnp.where(same & (second < first), 1.0, 0.0), 1, keepdims=True)
    rank_row = rank_row.astype(jnp.int32)
    rank_col = rank_col.astype(jnp.int32)
    local_col = jnp.clip(hub_col - part * vertex_rows, 0, vertex_rows - 1)
    ranks = lax.broadcasted_iota(jnp.int32, (HUB_MOST, hub_total), 0)
    selector = ((rank_row == ranks) & (owner_row == part)).astype(jnp.float32).astype(jnp.bfloat16)

    pl.semaphore_wait(barrier, greeted)

    exchanges = []
    for group in range(GROUPS):
        columns = pl.ds(group * group_rows, group_rows)
        exchanges.append(
            pltpu.make_async_remote_copy(
                src_ref=features_ref.at[:, columns], dst_ref=other_ref.at[:, columns],
                send_sem=feature_sems.at[0, group], recv_sem=feature_sems.at[1, group],
                device_id=(part, 1 - feat), device_id_type=MESH,
            )
        )
        exchanges[group].start()
    for group in range(GROUPS):
        rows = pl.ds(group * group_rows, group_rows)
        exchanges[group].wait_recv()
        projected = total_ref[:, rows] + over_rows(other_weight, other_ref[:, rows])
        projected = jnp.transpose(projected).astype(jnp.bfloat16)
        extended_ref[rows, :] = projected
        table_ref[:, group * width : (group + 1) * width] = projected

    candidates = picked_rows(local_col, table_ref, GROUPS)
    own_hubs = jnp.dot(selector, candidates, preferred_element_type=jnp.float32)
    own_hubs = own_hubs.astype(jnp.bfloat16)
    own_hubs_ref[...] = own_hubs
    hubs_ref[pl.ds(pl.multiple_of(part * HUB_MOST, 16), HUB_MOST), :] = own_hubs

    def hub_copy(number, first, blocks, target, source_ref=None):
        rows = pl.ds(pl.multiple_of(first * HUB_MOST, 16), blocks * HUB_MOST)
        return pltpu.make_async_remote_copy(
            src_ref=hubs_ref.at[rows, :] if source_ref is None else source_ref,
            dst_ref=hubs_ref.at[rows, :],
            send_sem=hub_send_sems.at[number], recv_sem=hub_receive_sems.at[number],
            device_id=(target, feat), device_id_type=MESH,
        )

    side = lax.rem(part, 2)
    across = part + 1 - 2 * side
    pair = part - side
    pair_side = lax.rem(part // 2, 2)
    far = part + 2 - 4 * pair_side
    far_pair = pair + 2 - 4 * pair_side
    plane = line * PLANE

    def line_copy(step, first):
        return hub_copy(1 + step, first, PLANE, lax.rem(part + step * PLANE, count))

    hub_copy(0, part, 1, across, own_hubs_ref).start()

    def halo_copy(slot):
        rows = pl.ds(vertex_rows + slot * half_rows, half_rows)
        return pltpu.make_async_remote_copy(
            src_ref=packed_ref.at[slot], dst_ref=extended_ref.at[rows, :],
            send_sem=send_sems.at[slot], recv_sem=receive_sems.at[slot],
            device_id=(lax.rem(part + offsets[slot] + count, count), feat), device_id_type=MESH,
        )

    chunk = math.gcd(half_rows, 512)
    order = sorted(range(slots), key=lambda slot: (abs(offsets[slot]) % 2 == 0, -abs(offsets[slot])))
    for number, slot in enumerate(order):
        if number == 2:
            hub_copy(0, across, 1, across, own_hubs_ref).wait_recv()
            hub_copy(1, pair, 2, far).start()
        if number == 5:
            hub_copy(1, far_pair, 2, far).wait_recv()
            for step in range(1, lines):
                line_copy(step, plane).start()
        target = part + offsets[slot]
        present = (target >= 0) & (target < count)

        @pl.when(present)
        def _():
            for start in range(0, half_rows, chunk):
                index = index_ref[start : start + chunk, slot : slot + 1]
                packed_ref[slot, start : start + chunk, :] = picked_rows(index, table_ref, GROUPS)
            halo_copy(slot).start()

        source = part - offsets[slot]

        @pl.when((source < 0) | (source >= count))
        def _():
            rows = pl.ds(vertex_rows + slot * half_rows, half_rows)
            extended_ref[rows, :] = jnp.zeros((half_rows, width), jnp.bfloat16)

    for step in range(1, lines):
        line_copy(step, lax.rem(line - step + lines, lines) * PLANE).wait_recv()
    place = owner_col * HUB_MOST + rank_col
    extended_ref[halo_end : halo_end + hub_total, :] = picked_rows(place, hubs_ref, 1)
    for exchange in exchanges:
        exchange.wait_send()
    hub_copy(0, part, 1, across, own_hubs_ref).wait_send()
    hub_copy(1, pair, 2, far).wait_send()
    for step in range(1, lines):
        line_copy(step, plane).wait_send()
    for slot in order:
        source = part - offsets[slot]
        target = part + offsets[slot]

        @pl.when((source >= 0) & (source < count))
        def _():
            halo_copy(slot).wait_recv()

        @pl.when((target >= 0) & (target < count))
        def _():
            halo_copy(slot).wait_send()


def tiles_kernel(
    rows_ref, cols_ref, count_ref, values_ref, extended_ref, bias_ref, out_ref, total_ref
):
    slots, edge, _ = values_ref.shape
    width = out_ref.shape[1]
    spare = out_ref.shape[0] // edge
    live = count_ref[0]
    total_ref[...] = jnp.zeros_like(total_ref)
    together = math.gcd(slots, 12)

    def step(number, carry):
        products, places = [], []
        for inner in range(together):
            slot = number * together + inner
            block = pl.ds(pl.multiple_of(cols_ref[slot] * edge, edge), edge)
            places.append(jnp.where(slot < live, rows_ref[slot], spare))
            products.append(
                jnp.dot(values_ref[slot], extended_ref[block, :], preferred_element_type=jnp.float32)
            )
        for place, product in zip(places, products):
            total_ref[pl.ds(pl.multiple_of(place * edge, edge), edge), :] += product
        return carry

    lax.fori_loop(0, (live + together - 1) // together, step, 0)
    summed = total_ref[: out_ref.shape[0], :] + bias_ref[...]
    out_ref[...] = jnp.maximum(summed, 0.0).astype(jnp.bfloat16)


def local(
    features, weight, out_bias, tile_values, tile_rows, tile_cols, tile_count, send_rows, hub_ids
):
    width = out_bias.shape[0]
    vertex_rows, depth = features.shape
    count = lax.axis_size("dom")
    _, slots, half_rows = send_rows.shape
    hub_total = hub_ids.shape[0]
    edge = tile_values.shape[1]
    vmem = pl.BlockSpec(memory_space=pltpu.VMEM)
    smem = pl.BlockSpec(memory_space=pltpu.SMEM)
    extended_rows = vertex_rows + slots * half_rows + hub_total
    extended = pl.pallas_call(
        functools.partial(exchange_kernel, count),
        out_shape=jax.ShapeDtypeStruct((extended_rows, width), jnp.bfloat16),
        in_specs=[vmem] * 4,
        out_specs=vmem,
        scratch_shapes=[
            pltpu.VMEM((depth, vertex_rows), jnp.bfloat16),
            pltpu.VMEM((width, vertex_rows), jnp.float32),
            pltpu.VMEM((vertex_rows // GROUPS, GROUPS * width), jnp.bfloat16),
            pltpu.VMEM((half_rows, slots), jnp.int32),
            pltpu.VMEM((slots, half_rows, width), jnp.bfloat16),
            pltpu.VMEM((HUB_MOST, width), jnp.bfloat16),
            pltpu.VMEM((count * HUB_MOST, width), jnp.bfloat16),
            pltpu.SemaphoreType.DMA((2, GROUPS)),
            pltpu.SemaphoreType.DMA((slots,)),
            pltpu.SemaphoreType.DMA((slots,)),
            pltpu.SemaphoreType.DMA((count // PLANE + 1,)),
            pltpu.SemaphoreType.DMA((count // PLANE + 1,)),
        ],
        compiler_params=pltpu.CompilerParams(
            collective_id=0, has_side_effects=True, vmem_limit_bytes=32 << 20
        ),
    )(jnp.transpose(features), weight, send_rows[0], hub_ids[None, :])
    return pl.pallas_call(
        tiles_kernel,
        out_shape=jax.ShapeDtypeStruct((vertex_rows, width), jnp.bfloat16),
        in_specs=[smem] * 3 + [vmem] * 3,
        out_specs=vmem,
        scratch_shapes=[pltpu.VMEM((vertex_rows + edge, width), jnp.float32)],
        compiler_params=pltpu.CompilerParams(vmem_limit_bytes=24 << 20),
    )(tile_rows, tile_cols, tile_count, tile_values, extended, out_bias[None, :])


def solution(mesh):
    in_specs = (
        P("dom", "feat"),
        P(),
        P("feat"),
        P("dom", None, None),
        P("dom"),
        P("dom"),
        P("dom"),
        P("dom", None, None),
        P(),
    )
    out_specs = P("dom", "feat")

    def program(features, weight, out_bias, *rest):
        whole_lanes = out_bias.shape[0] % (LANES * mesh.shape["feat"]) == 0
        fits = mesh.shape["feat"] == 2 and mesh.shape["dom"] % PLANE == 0
        body = local if fits and whole_lanes else local_any
        return jax.shard_map(
            body, mesh=mesh, in_specs=in_specs, out_specs=out_specs, check_vma=False
        )(features, weight, out_bias, *rest)

    return program
```

profile of v0, /device:TPU:12, one launch (start us, length us, event | category | flops | bytes accessed | tf_op | source)
XLA Modules:
  0.0 46.2 jit_solution(4779889438239934235)
XLA Ops:
  0.0 0.0 copy-start
  0.8 0.0 copy-start.1
  0.8 1.4 %copy-done.1 = bf16[2048,304]{0,1:T(8,128)(2,1)S(1)} copy-done((bf16[2048,304]{0,1:T(8,128)(2,1)S(1)}, bf16[2048,304]{0,1:T(8,128)(2,1)}, u32[]{:S(2)}) %copy-start.1) | copy-done | bytes 1245208
  2.3 0.0 copy-start.2
  2.3 1.0 %copy-done.2 = bf16[608,256]{1,0:T(8,128)(2,1)S(1)} copy-done((bf16[608,256]{1,0:T(8,128)(2,1)S(1)}, bf16[608,256]{1,0:T(8,128)(2,1)}, u32[]{:S(2)}) %copy-start.2) | copy-done | bytes 311320
  3.2 0.0 copy-start.3
  3.2 0.8 %copy-done.3 = s32[1,8,1024]{2,1,0:T(8,128)S(1)} copy-done((s32[1,8,1024]{2,1,0:T(8,128)S(1)}, s32[1,8,1024]{2,1,0:T(8,128)}, u32[]{:S(2)}) %copy-start.3) | copy-done | bytes 32792
  4.0 0.0 copy-start.4
  4.0 0.7 %copy-done.4 = s32[256]{0:T(256)S(1)} copy-done((s32[256]{0:T(256)S(1)}, s32[256]{0:T(256)}, u32[]{:S(2)}) %copy-start.4) | copy-done | bytes 1048
  4.7 0.0 copy-start.5
  4.7 0.0 copy-start.6
  4.7 0.0 copy-start.7
  4.7 37.5 %shard_map.91.extended_ref = bf16[10496,128]{1,0:T(8,128)(2,1)S(1)} custom-call(bf16[304,2048]{1,0:T(8,128)(2,1)S(1)} %bitcast.4, bf16[608,256]{1,0:T(8,128)(2,1)S(1)} %copy-done.2, s32[8,1024]{1,0:T(8,128)S(1)} %bitcast.5, s32[1,256]{1,0:T(1,128)S(1)} %bitcast.6), custom_call_target="tpu_custom_call" | custom-call | tf_op jit(solution)/shard_map/pallas_call | solution.py:310
  42.1 0.0 copy-done
  42.2 0.0 copy-done.5
  42.2 0.0 copy-done.6
  42.2 0.0 copy-done.7
  42.2 4.0 %shard_map.92 = bf16[2048,128]{1,0:T(8,128)(2,1)} custom-call(s32[108]{0:T(128)S(1)} %copy-done.5, s32[108]{0:T(128)S(1)} %copy-done.6, s32[1]{0:T(128)S(6)} %copy.10.count_ref, bf16[108,128,128]{2,1,0:T(8,128)(2,1)S(1)} %copy-done, bf16[10496,128]{1,0:T(8,128)(2,1)S(1)} %shard_map.91.extended_ref, f32[1,128]{1,0:T(1,128)S(1)} %bitcast.7), custom_call_target="tpu_custom_call" | custom-call | tf_op jit(solution)/shard_map/pallas_call | solution.py:333
Async XLA Ops:
  0.0 42.1 %copy-start = (bf16[108,128,128]{2,1,0:T(8,128)(2,1)S(1)}, bf16[108,128,128]{2,1,0:T(8,128)(2,1)}, u32[]{:S(2)}) copy-start(bf16[108,128,128]{2,1,0:T(8,128)(2,1)} %values_ref.1) | copy-start | bytes 10616836
  0.8 1.5 %copy-start.1 = (bf16[2048,304]{0,1:T(8,128)(2,1)S(1)}, bf16[2048,304]{0,1:T(8,128)(2,1)}, u32[]{:S(2)}) copy-start(bf16[2048,304]{0,1:T(8,128)(2,1)} %param.9) | copy-start | bytes 3735556
  2.3 1.0 %copy-start.2 = (bf16[608,256]{1,0:T(8,128)(2,1)S(1)}, bf16[608,256]{1,0:T(8,128)(2,1)}, u32[]{:S(2)}) copy-start(bf16[608,256]{1,0:T(8,128)(2,1)} %weight_ref.1) | copy-start | bytes 933892
  3.2 0.8 %copy-start.3 = (s32[1,8,1024]{2,1,0:T(8,128)S(1)}, s32[1,8,1024]{2,1,0:T(8,128)}, u32[]{:S(2)}) copy-start(s32[1,8,1024]{2,1,0:T(8,128)} %param.16) | copy-start | bytes 98308
  4.0 0.7 %copy-start.4 = (s32[256]{0:T(256)S(1)}, s32[256]{0:T(256)}, u32[]{:S(2)}) copy-start(s32[256]{0:T(256)} %param.17) | copy-start | bytes 3076
  4.7 37.5 %copy-start.5 = (s32[108]{0:T(128)S(1)}, s32[108]{0:T(128)}, u32[]{:S(2)}) copy-start(s32[108]{0:T(128)} %rows_ref.1) | copy-start | bytes 1300
  4.7 37.5 %copy-start.6 = (s32[108]{0:T(128)S(1)}, s32[108]{0:T(128)}, u32[]{:S(2)}) copy-start(s32[108]{0:T(128)} %cols_ref.1) | copy-start | bytes 1300
  4.7 37.5 %copy-start.7 = (f32[128]{0:T(128)S(1)}, f32[128]{0:T(128)}, u32[]{:S(2)}) copy-start(f32[128]{0:T(128)} %param.11) | copy-start | bytes 1540
where the time goes:
time: 46.7 us; the launch traced here: 46.2 us
  Pallas kernels  41.5 us (89%)
  local copies, waits for them, and re-layouts  3.87 us (8%)
  between operations  0.86 us (2%)
    pallas_call x1, Pallas kernels, local(): pl.pallas_call(functools.partial(exchange_kernel, count), out_shape=jax.S...  37.5 us
    pallas_call x1, Pallas kernels, local(): pl.pallas_call(tiles_kernel, out_shape=jax.ShapeDtypeStruct((vertex_rows,...  4 us
    unnamed x16, local copies, waits for them, and re-layouts  3.87 us

commit v1 on v0

--- a/solution.py
+++ b/solution.py
@@ -77,6 +77,7 @@
 LANES = 128
 GROUPS = 4
 PLANE = 4
+PIECES = 2
 MESH = pl.DeviceIdType.MESH
 
 
@@ -101,7 +102,8 @@
 
 
 def exchange_kernel(
-    count, features_ref, weight_ref, send_ref, hub_ref, extended_ref,
+    count, features_hbm, weight_hbm, send_hbm, hub_ref, extended_ref,
+    features_ref, weight_ref, send_ref, load_sems,
     other_ref, total_ref, table_ref, index_ref, packed_ref, own_hubs_ref, hubs_ref,
     feature_sems, send_sems, receive_sems, hub_send_sems, hub_receive_sems,
 ):
@@ -109,10 +111,17 @@
     feat = lax.axis_index("feat")
     depth, vertex_rows = features_ref.shape
     width = extended_ref.shape[1]
+    loads = []
+    for number, (source, target) in enumerate(
+        ((weight_hbm, weight_ref), (features_hbm, features_ref), (send_hbm, send_ref))
+    ):
+        loads.append(pltpu.make_async_copy(source, target, load_sems.at[number]))
+        loads[number].start()
     lines = count // PLANE
     line = part // PLANE
     group_rows = vertex_rows // GROUPS
     slots, half_rows = send_ref.shape
+    chunk = half_rows // PIECES
     offsets = list(range(-REACH, 0)) + list(range(1, REACH + 1))
     hub_total = hub_ref.shape[1]
     halo_end = vertex_rows + slots * half_rows
@@ -138,12 +147,6 @@
                 pl.semaphore_signal(
                     barrier, inc=1, device_id=(target, feat), device_id_type=MESH
                 )
-
-    columns = pl.ds(pl.multiple_of(feat * width, width), width)
-    own_weight = weight_ref[pl.ds(pl.multiple_of(feat * depth, 16), depth), columns]
-    other_weight = weight_ref[pl.ds(pl.multiple_of((1 - feat) * depth, 16), depth), columns]
-    total_ref[...] = over_rows(own_weight, features_ref[...])
-    index_ref[...] = jnp.transpose(send_ref[...])
 
     hub_row = hub_ref[...]
     hub_col = jnp.transpose(jnp.broadcast_to(hub_row, (8, hub_total)))[:, :1]
@@ -156,9 +159,18 @@
     rank_col = jnp.sum(jnp.where(same & (second < first), 1.0, 0.0), 1, keepdims=True)
     rank_row = rank_row.astype(jnp.int32)
     rank_col = rank_col.astype(jnp.int32)
-    local_col = jnp.clip(hub_col - part * vertex_rows, 0, vertex_rows - 1)
     ranks = lax.broadcasted_iota(jnp.int32, (HUB_MOST, hub_total), 0)
-    selector = ((rank_row == ranks) & (owner_row == part)).astype(jnp.float32).astype(jnp.bfloat16)
+    chosen = (rank_row == ranks) & (owner_row == part)
+    local_row = (hub_row - part * vertex_rows).astype(jnp.float32)
+    own_index = jnp.sum(jnp.where(chosen, local_row, 0.0), 1, keepdims=True).astype(jnp.int32)
+    loads[0].wait()
+    loads[1].wait()
+    columns = pl.ds(pl.multiple_of(feat * width, width), width)
+    own_weight = weight_ref[pl.ds(pl.multiple_of(feat * depth, 16), depth), columns]
+    other_weight = weight_ref[pl.ds(pl.multiple_of((1 - feat) * depth, 16), depth), columns]
+    total_ref[...] = over_rows(own_weight, features_ref[...])
+    loads[2].wait()
+    index_ref[...] = jnp.transpose(send_ref[...])
 
     pl.semaphore_wait(barrier, greeted)
 
@@ -167,7 +179,7 @@
         columns = pl.ds(group * group_rows, group_rows)
         exchanges.append(
             pltpu.make_async_remote_copy(
-                src_ref=features_ref.at[:, columns], dst_ref=other_ref.at[:, columns],
+                src_ref=features_hbm.at[:, columns], dst_ref=other_ref.at[:, columns],
                 send_sem=feature_sems.at[0, group], recv_sem=feature_sems.at[1, group],
                 device_id=(part, 1 - feat), device_id_type=MESH,
             )
@@ -181,9 +193,7 @@
         extended_ref[rows, :] = projected
         table_ref[:, group * width : (group + 1) * width] = projected
 
-    candidates = picked_rows(local_col, table_ref, GROUPS)
-    own_hubs = jnp.dot(selector, candidates, preferred_element_type=jnp.float32)
-    own_hubs = own_hubs.astype(jnp.bfloat16)
+    own_hubs = picked_rows(own_index, table_ref, GROUPS)
     own_hubs_ref[...] = own_hubs
     hubs_ref[pl.ds(pl.multiple_of(part * HUB_MOST, 16), HUB_MOST), :] = own_hubs
 
@@ -209,15 +219,14 @@
 
     hub_copy(0, part, 1, across, own_hubs_ref).start()
 
-    def halo_copy(slot):
-        rows = pl.ds(vertex_rows + slot * half_rows, half_rows)
+    def halo_copy(slot, piece):
+        rows = pl.ds(vertex_rows + slot * half_rows + piece * chunk, chunk)
         return pltpu.make_async_remote_copy(
-            src_ref=packed_ref.at[slot], dst_ref=extended_ref.at[rows, :],
-            send_sem=send_sems.at[slot], recv_sem=receive_sems.at[slot],
+            src_ref=packed_ref.at[slot, piece * chunk : (piece + 1) * chunk, :], dst_ref=extended_ref.at[rows, :],
+            send_sem=send_sems.at[slot, piece], recv_sem=receive_sems.at[slot, piece],
             device_id=(lax.rem(part + offsets[slot] + count, count), feat), device_id_type=MESH,
         )
 
-    chunk = math.gcd(half_rows, 512)
     order = sorted(range(slots), key=lambda slot: (abs(offsets[slot]) % 2 == 0, -abs(offsets[slot])))
     for number, slot in enumerate(order):
         if number == 2:
@@ -232,10 +241,11 @@
 
         @pl.when(present)
         def _():
-            for start in range(0, half_rows, chunk):
-                index = index_ref[start : start + chunk, slot : slot + 1]
-                packed_ref[slot, start : start + chunk, :] = picked_rows(index, table_ref, GROUPS)
-            halo_copy(slot).start()
+            for piece in range(PIECES):
+                rows = pl.ds(piece * chunk, chunk)
+                index = index_ref[rows, slot : slot + 1]
+                packed_ref[slot, rows, :] = picked_rows(index, table_ref, GROUPS)
+                halo_copy(slot, piece).start()
 
         source = part - offsets[slot]
 
@@ -260,11 +270,13 @@
 
         @pl.when((source >= 0) & (source < count))
         def _():
-            halo_copy(slot).wait_recv()
+            for piece in range(PIECES):
+                halo_copy(slot, piece).wait_recv()
 
         @pl.when((target >= 0) & (target < count))
         def _():
-            halo_copy(slot).wait_send()
+            for piece in range(PIECES):
+                halo_copy(slot, piece).wait_send()
 
 
 def tiles_kernel(
@@ -310,9 +322,13 @@
     extended = pl.pallas_call(
         functools.partial(exchange_kernel, count),
         out_shape=jax.ShapeDtypeStruct((extended_rows, width), jnp.bfloat16),
-        in_specs=[vmem] * 4,
+        in_specs=[pl.BlockSpec(memory_space=pltpu.HBM)] * 3 + [vmem],
         out_specs=vmem,
         scratch_shapes=[
+            pltpu.VMEM((depth, vertex_rows), jnp.bfloat16),
+            pltpu.VMEM(weight.shape, jnp.bfloat16),
+            pltpu.VMEM((slots, half_rows), jnp.int32),
+            pltpu.SemaphoreType.DMA((3,)),
             pltpu.VMEM((depth, vertex_rows), jnp.bfloat16),
             pltpu.VMEM((width, vertex_rows), jnp.float32),
             pltpu.VMEM((vertex_rows // GROUPS, GROUPS * width), jnp.bfloat16),
@@ -321,8 +337,8 @@
             pltpu.VMEM((HUB_MOST, width), jnp.bfloat16),
             pltpu.VMEM((count * HUB_MOST, width), jnp.bfloat16),
             pltpu.SemaphoreType.DMA((2, GROUPS)),
-            pltpu.SemaphoreType.DMA((slots,)),
-            pltpu.SemaphoreType.DMA((slots,)),
+            pltpu.SemaphoreType.DMA((slots, PIECES)),
+            pltpu.SemaphoreType.DMA((slots, PIECES)),
             pltpu.SemaphoreType.DMA((count // PLANE + 1,)),
             pltpu.SemaphoreType.DMA((count // PLANE + 1,)),
         ],

time: 46.7 us -> 46.6 us (level)
  no operation moved by 1% of the time
where the time goes in v1:
time: 46.6 us; the launch traced here: 46.1 us
  Pallas kernels  41.4 us (89%)
  local copies, waits for them, and re-layouts  3.87 us (8%)
  between operations  0.86 us (2%)
    pallas_call x1, Pallas kernels, local(): pl.pallas_call(functools.partial(exchange_kernel, count), out_shape=jax.S...  37.4 us
    pallas_call x1, Pallas kernels, local(): pl.pallas_call(tiles_kernel, out_shape=jax.ShapeDtypeStruct((vertex_rows,...  3.97 us
    unnamed x16, local copies, waits for them, and re-layouts  3.87 us

profile of v1, /device:TPU:12, one launch (start us, length us, event | category | flops | bytes accessed | tf_op | source)
XLA Modules:
  0.0 46.1 jit_solution(8438306379774273769)
XLA Ops:
  0.0 0.0 copy-start
  0.8 0.0 copy-start.1
  0.8 1.4 %copy-done.1 = bf16[2048,304]{0,1:T(8,128)(2,1)S(1)} copy-done((bf16[2048,304]{0,1:T(8,128)(2,1)S(1)}, bf16[2048,304]{0,1:T(8,128)(2,1)}, u32[]{:S(2)}) %copy-start.1) | copy-done | bytes 1245208
  2.3 0.0 copy-start.2
  2.3 1.0 %copy-done.2 = bf16[608,256]{1,0:T(8,128)(2,1)S(1)} copy-done((bf16[608,256]{1,0:T(8,128)(2,1)S(1)}, bf16[608,256]{1,0:T(8,128)(2,1)}, u32[]{:S(2)}) %copy-start.2) | copy-done | bytes 311320
  3.2 0.0 copy-start.3
  3.2 0.8 %copy-done.3 = s32[1,8,1024]{2,1,0:T(8,128)S(1)} copy-done((s32[1,8,1024]{2,1,0:T(8,128)S(1)}, s32[1,8,1024]{2,1,0:T(8,128)}, u32[]{:S(2)}) %copy-start.3) | copy-done | bytes 32792
  4.0 0.0 copy-start.4
  4.0 0.7 %copy-done.4 = s32[256]{0:T(256)S(1)} copy-done((s32[256]{0:T(256)S(1)}, s32[256]{0:T(256)}, u32[]{:S(2)}) %copy-start.4) | copy-done | bytes 1048
  4.7 0.0 copy-start.5
  4.7 0.0 copy-start.6
  4.7 0.0 copy-start.7
  4.7 37.4 %shard_map.91.extended_ref = bf16[10496,128]{1,0:T(8,128)(2,1)S(1)} custom-call(bf16[304,2048]{1,0:T(8,128)(2,1)S(1)} %bitcast.4, bf16[608,256]{1,0:T(8,128)(2,1)S(1)} %copy-done.2, s32[8,1024]{1,0:T(8,128)S(1)} %bitcast.5, s32[1,256]{1,0:T(1,128)S(1)} %bitcast.6), custom_call_target="tpu_custom_call" | custom-call | tf_op jit(solution)/shard_map/pallas_call | solution.py:322
  42.1 0.0 copy-done
  42.1 0.0 copy-done.5
  42.1 0.0 copy-done.6
  42.1 0.0 copy-done.7
  42.1 4.0 %shard_map.92 = bf16[2048,128]{1,0:T(8,128)(2,1)} custom-call(s32[108]{0:T(128)S(1)} %copy-done.5, s32[108]{0:T(128)S(1)} %copy-done.6, s32[1]{0:T(128)S(6)} %copy.10.count_ref, bf16[108,128,128]{2,1,0:T(8,128)(2,1)S(1)} %copy-done, bf16[10496,128]{1,0:T(8,128)(2,1)S(1)} %shard_map.91.extended_ref, f32[1,128]{1,0:T(1,128)S(1)} %bitcast.7), custom_call_target="tpu_custom_call" | custom-call | tf_op jit(solution)/shard_map/pallas_call | solution.py:349
Async XLA Ops:
  0.0 42.1 %copy-start = (bf16[108,128,128]{2,1,0:T(8,128)(2,1)S(1)}, bf16[108,128,128]{2,1,0:T(8,128)(2,1)}, u32[]{:S(2)}) copy-start(bf16[108,128,128]{2,1,0:T(8,128)(2,1)} %values_ref.1) | copy-start | bytes 10616836
  0.8 1.5 %copy-start.1 = (bf16[2048,304]{0,1:T(8,128)(2,1)S(1)}, bf16[2048,304]{0,1:T(8,128)(2,1)}, u32[]{:S(2)}) copy-start(bf16[2048,304]{0,1:T(8,128)(2,1)} %param.9) | copy-start | bytes 3735556
  2.3 1.0 %copy-start.2 = (bf16[608,256]{1,0:T(8,128)(2,1)S(1)}, bf16[608,256]{1,0:T(8,128)(2,1)}, u32[]{:S(2)}) copy-start(bf16[608,256]{1,0:T(8,128)(2,1)} %weight_hbm.1) | copy-start | bytes 933892
  3.2 0.8 %copy-start.3 = (s32[1,8,1024]{2,1,0:T(8,128)S(1)}, s32[1,8,1024]{2,1,0:T(8,128)}, u32[]{:S(2)}) copy-start(s32[1,8,1024]{2,1,0:T(8,128)} %param.16) | copy-start | bytes 98308
  4.0 0.7 %copy-start.4 = (s32[256]{0:T(256)S(1)}, s32[256]{0:T(256)}, u32[]{:S(2)}) copy-start(s32[256]{0:T(256)} %param.17) | copy-start | bytes 3076
  4.7 37.5 %copy-start.5 = (s32[108]{0:T(128)S(1)}, s32[108]{0:T(128)}, u32[]{:S(2)}) copy-start(s32[108]{0:T(128)} %rows_ref.1) | copy-start | bytes 1300
  4.7 37.5 %copy-start.6 = (s32[108]{0:T(128)S(1)}, s32[108]{0:T(128)}, u32[]{:S(2)}) copy-start(s32[108]{0:T(128)} %cols_ref.1) | copy-start | bytes 1300
  4.7 37.5 %copy-start.7 = (f32[128]{0:T(128)S(1)}, f32[128]{0:T(128)}, u32[]{:S(2)}) copy-start(f32[128]{0:T(128)} %param.11) | copy-start | bytes 1540
